TPU v7x, 512 devices: a whole 4x8x8 slice. The times are simulated.
512 devices in a mesh: pb: 8 (over y_lo, x), ka: 16 (over z, core), ha: 4 (over y_hi).
Axes of the slice: x: 4, y: 8 (y_hi: 4, y_lo: 2; y = y_hi * 2 + y_lo), z: 8, core: 2. Of those that a mesh axis runs over, the one named last changes fastest.
Arguments:
- queries: bfloat16 [3072, 64, 128], P('pb', 'ha'), may hold values from -6 to 6
- key_codes: bfloat16 [3072, 8, 128], P('ka', 'ha'), may hold values from -4 to 4
- key_scale_powers: int32 [48, 8], P('ka', 'ha'), may hold values from -1 to 1
- values: bfloat16 [3072, 8, 128], P('ka', 'ha'), may hold values from -6 to 6
- grad_out: bfloat16 [3072, 64, 128], P('pb', 'ha'), may hold values from -1.5 to 1.5
- grad_dot: float32 [3072, 64], P('pb', 'ha'), may hold values from -6 to 6
- log_totals: float32 [3072, 64], P('pb', 'ha')
Outputs:
- grad_queries: bfloat16 [3072, 64, 128], P(('pb', 'ka'), 'ha')
- grad_keys: bfloat16 [3072, 8, 128], P('ka', 'ha')
- grad_values: bfloat16 [3072, 8, 128], P('ka', 'ha')
All inputs are finite; a program needn't handle non-finite values.
Results may differ from a plain program's by a relative error of at most 0.012.
Values may be sent and summed in bfloat16 or wider, within the bound.
A program may use at most 64 MiB of HBM per device.

v0:
```python
import jax
import jax.numpy as jnp
from jax import lax
from jax.sharding import PartitionSpec as P

KEYS_PER_SCALE = 64


def copy_for_each(array, axis):
    peers = lax.axis_size(axis)
    return lax.all_to_all(
        jnp.broadcast_to(array[None], (peers, *array.shape)), axis, 0, 0, tiled=True
    )


def over_copies(array, axis):
    return copy_for_each(array, axis).sum(axis=0)


def cut_along(array, dim, peers):
    before, after = (array.shape[:dim], array.shape[dim + 1 :])
    return jnp.moveaxis(array.reshape(*before, peers, -1, *after), dim, 0)


def sum_at_owner(array, axis, dim):
    pieces = cut_along(array, dim, lax.axis_size(axis))
    arrived = lax.all_to_all(pieces, axis, split_axis=0, concat_axis=0, tiled=True)
    return arrived.astype(jnp.float32).sum(axis=0)


def over_copies_2(array, axis):
    return copy_for_each(array, axis).astype(jnp.float32).sum(axis=0)


def head_grads(
    query_block, grad_block, dot_block, total_block, key_block, value_block, query_pos, key_pos
):
    inverse_root = query_block.shape[-1] ** (-0.5)
    scores = (
        jnp.einsum("igd,jd->gij", query_block, key_block, preferred_element_type=jnp.float32)
        * inverse_root
    )
    visible = key_pos[None, :] <= query_pos[:, None]
    weights = jnp.where(visible[None], jnp.exp(scores - total_block.T[:, :, None]), 0.0)
    weights_low = weights.astype(jnp.bfloat16)
    grad_values = jnp.einsum(
        "gij,igd->jd", weights_low, grad_block, preferred_element_type=jnp.float32
    )
    grad_weights = jnp.einsum(
        "igd,jd->gij", grad_block, value_block, preferred_element_type=jnp.float32
    )
    grad_scores = (weights * (grad_weights - dot_block.T[:, :, None])).astype(jnp.bfloat16)
    grad_query = (
        jnp.einsum("gij,jd->igd", grad_scores, key_block, preferred_element_type=jnp.float32)
        * inverse_root
    )
    grad_keys = (
        jnp.einsum("gij,igd->jd", grad_scores, query_block, preferred_element_type=jnp.float32)
        * inverse_root
    )
    return (grad_query, grad_keys, grad_values)


def per_device(queries, key_codes, key_scale_powers, values, grad_out, grad_dot, log_totals):
    query_count, head_count, head_width = queries.shape
    key_count, kv_heads, _ = key_codes.shape
    queries_per_group = head_count // kv_heads
    key_devices = lax.axis_size("ka")
    factor = jnp.exp2(key_scale_powers.astype(jnp.float32))
    dequantized = (
        key_codes.astype(jnp.float32) * jnp.repeat(factor, KEYS_PER_SCALE, axis=0)[:, :, None]
    )
    key_total = over_copies(jnp.sum(dequantized, axis=0), "ka")
    smoothed = (dequantized - key_total / (key_count * key_devices)).astype(jnp.bfloat16)
    query_in, grads_in, dots_in, totals_in = (queries, grad_out, grad_dot, log_totals)
    keys_in, values_in = (smoothed, values)
    query_pos = lax.axis_index("pb") * query_count + lax.iota(jnp.int32, query_count)
    key_pos = lax.axis_index("ka") * key_count + lax.iota(jnp.int32, key_count)
    blocks = ((0, 0),)
    halves = 1
    outer = 1
    query_step = query_count // halves
    key_step = key_count // halves
    query_parts = []
    key_parts = []
    value_parts = []
    for kv_head in range(kv_heads):
        chosen = slice(kv_head * queries_per_group, (kv_head + 1) * queries_per_group)
        query_sums = [None] * halves
        key_sums_local = [None] * halves
        value_sums = [None] * halves
        query_half, key_half = blocks[0]
        query_range = slice(query_half * query_step, (query_half + 1) * query_step)
        key_range = slice(key_half * key_step, (key_half + 1) * key_step)
        part_query, part_keys, part_values = head_grads(
            query_in[query_range, chosen],
            grads_in[query_range, chosen],
            dots_in[query_range, chosen],
            totals_in[query_range, chosen],
            keys_in[key_range, kv_head],
            values_in[key_range, kv_head],
            query_pos,
            key_pos,
        )
        query_sums[query_half] = part_query
        key_sums_local[key_half] = part_keys
        value_sums[key_half] = part_values
        query_parts.append(query_sums[0])
        key_parts.append(key_sums_local[0])
        value_parts.append(value_sums[0])
    grad_query = jnp.concatenate(query_parts, axis=1)
    grad_keys = jnp.stack(key_parts, axis=1)
    grad_values = jnp.stack(value_parts, axis=1)
    share = query_count // key_devices
    summed = sum_at_owner(
        grad_query.reshape(outer, key_devices, share // outer, head_count, head_width).astype(
            jnp.bfloat16
        ),
        "ka",
        1,
    )
    key_sum, value_sum = (
        over_copies_2(grad_keys.astype(jnp.bfloat16), "pb").astype(jnp.float32),
        over_copies_2(grad_values.astype(jnp.bfloat16), "pb").astype(jnp.float32),
    )
    query_out = summed.reshape(share, head_count, head_width).astype(jnp.bfloat16)
    keys_out = key_sum.astype(jnp.bfloat16)
    values_out = value_sum.astype(jnp.bfloat16)
    return (query_out, keys_out, values_out)


def solution(mesh):
    in_specs = (
        P("pb", "ha", None),
        P("ka", "ha", None),
        P("ka", "ha"),
        P("ka", "ha", None),
        P("pb", "ha", None),
        P("pb", "ha"),
        P("pb", "ha"),
    )
    out_specs = (P(("pb", "ka"), "ha", None), P("ka", "ha", None), P("ka", "ha", None))
    return jax.shard_map(
        per_device, mesh=mesh, in_specs=in_specs, out_specs=out_specs, check_vma=False
    )
```

profile of v0, /device:TPU:1, one launch (start us, length us, event | category | flops | bytes accessed | tf_op | source)
XLA Modules:
  0.0 105.1 jit_solution(7809879326718569404)
XLA Ops:
  0.6 0.0 copy-start.3
  0.6 0.8 multiply_exponential_fusion
  1.4 0.1 broadcast_in_dim.24
  1.5 0.1 mul.52
  1.6 1.0 fusion.52
  2.6 0.6 broadcast_in_dim.25
  3.2 11.8 %all-to-all-start = ((f32[16,2,128]{2,1,0:T(2,128)}), f32[16,2,128]{2,1,0:T(2,128)S(1)}, u32[]{:S(2)}, u32[]{:S(2)}) async-start(f32[16,2,128]{2,1,0:T(2,128)} %broadcast_in_dim.25), calls=%async_computation | async-start | bytes 32768 | tf_op jit(solution)/shard_map/all_to_all | solution.py:11
  15.1 1.5 %fusion.58 = (bf16[384,8,128]{2,1,0:T(8,128)(2,1)S(1)}, bf16[384,8,128]{2,1,0:T(8,128)(2,1)S(1)}) fusion(bf16[384,16,128]{2,1,0:T(8,128)(2,1)} %param.7), kind=kLoop, calls=%fused_computation.70 | loop fusion | bytes 3145728 | tf_op jit(solution)/shard_map/slice | solution.py:96
  16.6 0.0 copy-done.3
  16.6 0.0 copy-start.12
  16.6 0.0 copy-start.13
  16.6 0.0 copy-start.10
  16.6 1.2 %fusion.57 = (bf16[384,8,128]{2,1,0:T(8,128)(2,1)}, bf16[384,8,128]{2,1,0:T(8,128)(2,1)}) fusion(bf16[384,16,128]{2,1,0:T(8,128)(2,1)S(1)} %copy-done.3), kind=kLoop, calls=%fused_computation.69 | loop fusion | bytes 3145728 | tf_op jit(solution)/shard_map/slice | solution.py:97
  17.9 0.1 broadcast_compare_fusion
  18.0 0.0 copy-done.12
  18.0 0.0 copy-done.13
  18.0 4.4 %all-to-all-done = f32[16,2,128]{2,1,0:T(2,128)S(1)} async-done(((f32[16,2,128]{2,1,0:T(2,128)}), f32[16,2,128]{2,1,0:T(2,128)S(1)}, u32[]{:S(2)}, u32[]{:S(2)}) %all-to-all-start) | async-done | bytes 16416 | tf_op jit(solution)/shard_map/all_to_all | solution.py:11
  22.4 0.0 copy-done.10
  22.4 0.1 subtract_convert_fusion
  22.6 0.5 fusion.50
  23.0 0.0 copy-start.2
  23.1 0.0 copy-start.9
  23.1 0.5 fusion.45
  23.5 0.0 copy-start
  23.6 0.0 copy-start.8
  23.6 1.2 %copy-done.9 = bf16[384,8,128]{2,1,0:T(8,128)(2,1)S(1)} copy-done((bf16[384,8,128]{2,1,0:T(8,128)(2,1)S(1)}, bf16[384,8,128]{2,1,0:T(8,128)(2,1)}, u32[]{:S(2)}) %copy-start.9) | copy-done | bytes 786456
  24.8 0.7 fusion.34
  25.4 0.2 copy-done.8
  25.6 0.7 fusion.37
  26.3 0.0 copy-done
  26.3 0.0 copy-start.11
  26.3 0.0 copy-done.2
  26.3 1.1 %broadcast_in_dim.29 = bf16[8,192,2,128]{3,1,2,0:T(8,128)(2,1)} broadcast(bf16[192,2,128]{2,0,1:T(8,128)(2,1)S(1)} %pad_maximum_fusion.2), dimensions={1,2,3} | broadcast | bytes 884736 | tf_op jit(solution)/shard_map/broadcast_in_dim | solution.py:12
  27.4 5.0 %all-to-all-start.3 = ((bf16[8,192,2,128]{3,1,2,0:T(8,128)(2,1)}), bf16[8,192,2,128]{3,1,2,0:T(8,128)(2,1)S(1)}, u32[]{:S(2)}, u32[]{:S(2)}) async-start(bf16[8,192,2,128]{3,1,2,0:T(8,128)(2,1)} %broadcast_in_dim.29), calls=%async_computation.3 | async-start | bytes 1572864 | tf_op jit(solution)/shard_map/all_to_all | solution.py:11
  32.4 0.0 copy-done.11
  32.4 0.1 fusion.59
  32.5 0.0 copy-start.1
  32.6 2.9 %fusion.5 = bf16[8,384,192]{1,2,0:T(8,128)(2,1)S(1)} fusion(f32[192,384,8]{1,0,2:T(8,128)} %copy-done.2, f32[8,384]{1,0:T(8,128)S(1)} %get-tuple-element.17, f32[8,384]{1,0:T(8,128)S(1)} %get-tuple-element.20, pred[384,192]{0,1:T(8,128)(4,1)S(1)} %broadcast_compare_fusion, bf16[384,8,128]{2,1,0:T(8,128)(2,1)} %get-tuple-element.9, ...), kind=kOutput, calls=%fused_computation.8 | convolution fusion | flops 154533888 | bytes 4472832 | tf_op jit(solution)/shard_map/igd,jd->gij/dot_general | solution.py:49
  35.5 0.0 copy-start.4
  35.5 0.5 fusion.41
  36.0 0.0 copy-done.1
  36.0 0.9 fusion.1
  36.9 0.0 copy-done.4
  37.0 0.0 copy-start.6
  37.0 0.5 fusion.40
  37.4 0.5 copy-done.6
  38.0 6.2 %all-to-all-done.3 = bf16[8,192,2,128]{3,1,2,0:T(8,128)(2,1)S(1)} async-done(((bf16[8,192,2,128]{3,1,2,0:T(8,128)(2,1)}), bf16[8,192,2,128]{3,1,2,0:T(8,128)(2,1)S(1)}, u32[]{:S(2)}, u32[]{:S(2)}) %all-to-all-start.3) | async-done | bytes 786464 | tf_op jit(solution)/shard_map/all_to_all | solution.py:11
  44.2 1.0 broadcast_in_dim.28
  45.2 4.0 %all-to-all-start.2 = ((bf16[8,192,2,128]{3,1,2,0:T(8,128)(2,1)}), bf16[8,192,2,128]{3,1,2,0:T(8,128)(2,1)S(1)}, u32[]{:S(2)}, u32[]{:S(2)}) async-start(bf16[8,192,2,128]{3,1,2,0:T(8,128)(2,1)} %broadcast_in_dim.28), calls=%async_computation.2 | async-start | bytes 1572864 | tf_op jit(solution)/shard_map/all_to_all | solution.py:11
  49.2 0.0 copy-done.5
  49.2 0.0 copy-start.7
  49.2 0.4 fusion.10
  49.6 0.9 copy-done.7
  50.5 0.4 fusion.11
  50.9 0.2 pad_maximum_fusion
  51.1 2.0 %copy.59 = bf16[384,16,128]{2,1,0:T(8,128)(2,1)} copy(bf16[384,16,128]{0,2,1:T(8,128)(2,1)S(1)} %pad_maximum_fusion) | data formatting | bytes 3145728 | tf_op jit(solution)/shard_map/concatenate | solution.py:111
  53.1 7.9 %all-to-all-done.2 = bf16[8,192,2,128]{3,1,2,0:T(8,128)(2,1)S(1)} async-done(((bf16[8,192,2,128]{3,1,2,0:T(8,128)(2,1)}), bf16[8,192,2,128]{3,1,2,0:T(8,128)(2,1)S(1)}, u32[]{:S(2)}, u32[]{:S(2)}) %all-to-all-start.2) | async-done | bytes 786464 | tf_op jit(solution)/shard_map/all_to_all | solution.py:11
  61.0 4.7 %all-to-all-start.1 = ((bf16[16,1,1,24,16,128]{5,4,3,2,1,0:T(8,128)(2,1)}), bf16[16,1,1,24,16,128]{5,4,3,2,1,0:T(8,128)(2,1)S(1)}, u32[]{:S(2)}, u32[]{:S(2)}) async-start(bf16[16,1,1,24,16,128]{5,4,3,2,1,0:T(8,128)(2,1)} %bitcast.19), calls=%async_computation.1 | async-start | bytes 3145728 | tf_op jit(solution)/shard_map/all_to_all | solution.py:27
  65.7 0.1 reduce_sum.58
  65.8 0.7 copy.62
  66.5 0.1 reduce_sum.57
  66.6 0.7 copy.61
  67.4 36.9 %all-to-all-done.1 = bf16[16,1,1,24,16,128]{5,4,3,2,1,0:T(8,128)(2,1)S(1)} async-done(((bf16[16,1,1,24,16,128]{5,4,3,2,1,0:T(8,128)(2,1)}), bf16[16,1,1,24,16,128]{5,4,3,2,1,0:T(8,128)(2,1)S(1)}, u32[]{:S(2)}, u32[]{:S(2)}) %all-to-all-start.1) | async-done | bytes 1572896 | tf_op jit(solution)/shard_map/all_to_all | solution.py:27
  104.2 0.9 reduce_sum.56
  (8 shorter events, 0.1 us)
Async XLA Ops:
  0.6 15.9 %copy-start.3 = (bf16[384,16,128]{2,1,0:T(8,128)(2,1)S(1)}, bf16[384,16,128]{2,1,0:T(8,128)(2,1)}, u32[]{:S(2)}) copy-start(bf16[384,16,128]{2,1,0:T(8,128)(2,1)} %param.11) | copy-start | bytes 4718596
  3.2 19.2 %all-to-all-start = ((f32[16,2,128]{2,1,0:T(2,128)}), f32[16,2,128]{2,1,0:T(2,128)S(1)}, u32[]{:S(2)}, u32[]{:S(2)}) async-start(f32[16,2,128]{2,1,0:T(2,128)} %broadcast_in_dim.25), calls=%async_computation | async-start | bytes 32768 | tf_op jit(solution)/shard_map/all_to_all | solution.py:11
  16.6 1.4 %copy-start.12 = (f32[384,16]{0,1:T(8,128)S(1)}, f32[384,16]{0,1:T(8,128)}, u32[]{:S(2)}) copy-start(f32[384,16]{0,1:T(8,128)} %param.12) | copy-start | bytes 73732
  16.6 1.4 %copy-start.13 = (f32[384,16]{0,1:T(8,128)S(1)}, f32[384,16]{0,1:T(8,128)}, u32[]{:S(2)}) copy-start(f32[384,16]{0,1:T(8,128)} %param.13) | copy-start | bytes 73732
  16.6 5.8 %copy-start.10 = (bf16[192,2,128]{2,1,0:T(2,128)(2,1)S(1)}, bf16[192,2,128]{2,1,0:T(2,128)(2,1)}, u32[]{:S(2)}) copy-start(bf16[192,2,128]{2,1,0:T(2,128)(2,1)} %param.8) | copy-start | bytes 294916
  23.0 3.3 %copy-start.2 = (f32[192,384,8]{1,0,2:T(8,128)}, f32[192,384,8]{1,0,2:T(8,128)S(1)}, u32[]{:S(2)}) copy-start(f32[192,384,8]{1,0,2:T(8,128)S(1)} %fusion.50) | copy-start | bytes 7077892
  23.1 1.7 %copy-start.9 = (bf16[384,8,128]{2,1,0:T(8,128)(2,1)S(1)}, bf16[384,8,128]{2,1,0:T(8,128)(2,1)}, u32[]{:S(2)}) copy-start(bf16[384,8,128]{2,1,0:T(8,128)(2,1)} %get-tuple-element.9) | copy-start | bytes 2359300
  23.5 2.7 %copy-start = (f32[192,384,8]{1,0,2:T(8,128)}, f32[192,384,8]{1,0,2:T(8,128)S(1)}, u32[]{:S(2)}) copy-start(f32[192,384,8]{1,0,2:T(8,128)S(1)} %fusion.45) | copy-start | bytes 7077892
  23.6 2.0 %copy-start.8 = (bf16[384,8,128]{2,1,0:T(8,128)(2,1)S(1)}, bf16[384,8,128]{2,1,0:T(8,128)(2,1)}, u32[]{:S(2)}) copy-start(bf16[384,8,128]{2,1,0:T(8,128)(2,1)} %get-tuple-element.10) | copy-start | bytes 2359300
  26.3 6.1 %copy-start.11 = (bf16[192,2,128]{2,1,0:T(2,128)(2,1)S(1)}, bf16[192,2,128]{2,1,0:T(2,128)(2,1)}, u32[]{:S(2)}) copy-start(bf16[192,2,128]{2,1,0:T(2,128)(2,1)} %param.10) | copy-start | bytes 294916
  27.4 16.9 %all-to-all-start.3 = ((bf16[8,192,2,128]{3,1,2,0:T(8,128)(2,1)}), bf16[8,192,2,128]{3,1,2,0:T(8,128)(2,1)S(1)}, u32[]{:S(2)}, u32[]{:S(2)}) async-start(bf16[8,192,2,128]{3,1,2,0:T(8,128)(2,1)} %broadcast_in_dim.29), calls=%async_computation.3 | async-start | bytes 1572864 | tf_op jit(solution)/shard_map/all_to_all | solution.py:11
  32.5 3.4 %copy-start.1 = (f32[192,384,8]{1,0,2:T(8,128)S(1)}, f32[192,384,8]{1,0,2:T(8,128)}, u32[]{:S(2)}) copy-start(f32[192,384,8]{1,0,2:T(8,128)} %copy-done) | copy-start | bytes 7077892
  35.5 1.4 %copy-start.4 = (bf16[8,384,192]{1,2,0:T(8,128)(2,1)}, bf16[8,384,192]{1,2,0:T(8,128)(2,1)S(1)}, u32[]{:S(2)}) copy-start(bf16[8,384,192]{1,2,0:T(8,128)(2,1)S(1)} %fusion.5) | copy-start | bytes 3538948
  37.0 1.0 copy-start.6
  38.0 11.3 %copy-start.5 = (bf16[8,384,192]{1,2,0:T(8,128)(2,1)S(1)}, bf16[8,384,192]{1,2,0:T(8,128)(2,1)}, u32[]{:S(2)}) copy-start(bf16[8,384,192]{1,2,0:T(8,128)(2,1)} %copy-done.4) | copy-start | bytes 3538948
  45.2 15.7 %all-to-all-start.2 = ((bf16[8,192,2,128]{3,1,2,0:T(8,128)(2,1)}), bf16[8,192,2,128]{3,1,2,0:T(8,128)(2,1)S(1)}, u32[]{:S(2)}, u32[]{:S(2)}) async-start(bf16[8,192,2,128]{3,1,2,0:T(8,128)(2,1)} %broadcast_in_dim.28), calls=%async_computation.2 | async-start | bytes 1572864 | tf_op jit(solution)/shard_map/all_to_all | solution.py:11
  49.2 1.3 %copy-start.7 = (bf16[8,384,192]{1,2,0:T(8,128)(2,1)S(1)}, bf16[8,384,192]{1,2,0:T(8,128)(2,1)}, u32[]{:S(2)}) copy-start(bf16[8,384,192]{1,2,0:T(8,128)(2,1)} %copy-done.6) | copy-start | bytes 3538948
  61.0 43.3 %all-to-all-start.1 = ((bf16[16,1,1,24,16,128]{5,4,3,2,1,0:T(8,128)(2,1)}), bf16[16,1,1,24,16,128]{5,4,3,2,1,0:T(8,128)(2,1)S(1)}, u32[]{:S(2)}, u32[]{:S(2)}) async-start(bf16[16,1,1,24,16,128]{5,4,3,2,1,0:T(8,128)(2,1)} %bitcast.19), calls=%async_computation.1 | async-start | bytes 3145728 | tf_op jit(solution)/shard_map/all_to_all | solution.py:27
where the time goes:
time: 106 us; the launch traced here: 105 us
  waiting for transfers between devices  55.4 us (52%)
  starting transfers between devices  25.5 us (24%)
  local copies, waits for them, and re-layouts  12 us (11%)
  matrix products  7.85 us (7%)
  other arithmetic  3.38 us (3%)
    all_to_all x1, waiting for transfers between devices, sum_at_owner(): lax.all_to_all(pieces, axis, split_axis=0, concat_axis=0, tiled=True)  36.9 us
    all_to_all x3, starting transfers between devices, copy_for_each(): lax.all_to_all(jnp.broadcast_to(array[None], (peers, *array.shape)), axis...  20.8 us
    all_to_all x3, waiting for transfers between devices, copy_for_each(): lax.all_to_all(jnp.broadcast_to(array[None], (peers, *array.shape)), axis...  18.5 us
    all_to_all x1, starting transfers between devices, sum_at_owner(): lax.all_to_all(pieces, axis, split_axis=0, concat_axis=0, tiled=True)  4.71 us
    unnamed x30, local copies, waits for them, and re-layouts  4.3 us
    dot_general x2, matrix products, head_grads(): jnp.einsum('igd,jd->gij', grad_block, value_block, preferred_element_type...  3.87 us
    broadcast_in_dim x3, local copies, waits for them, and re-layouts, copy_for_each(): jnp.broadcast_to(array[None], (peers, *array.shape))  2.7 us
  transfers between devices with their start and end apart: 4, of which 4 were waited for; matrix products, arithmetic and copies ran while one was open for 12% of the time, Pallas kernels for 0%

commit v1 on v0

v1 whole, which is shorter than its diff:
```python
import functools

import jax
import jax.numpy as jnp
from jax import lax
from jax.experimental import pallas as pl
from jax.experimental.pallas import tpu as pltpu
from jax.sharding import PartitionSpec as P

F32 = jnp.float32
BF16 = jnp.bfloat16
MESH = pl.DeviceIdType.MESH
NT = (((1,), (1,)), ((), ()))
NN = (((1,), (0,)), ((), ()))

PB = 8
NZ = 8
KA = 16
TOK = 384
GROUP = 8
D = 128
KEYS = 192
CKEYS = 384
SHARE = 48
ROWS = SHARE * GROUP
HALF = ROWS // 2
PIECE = CKEYS // PB
KEYS_PER_SCALE = 64
LOG2E = 1.4426950408889634


def dot(a, b, dims):
    return lax.dot_general(a, b, dims, preferred_element_type=F32)


def split3(x):
    hi = x.astype(BF16).astype(F32)
    rest = x - hi
    mid = rest.astype(BF16).astype(F32)
    return hi, mid, rest - mid


def kernel(
    q_hbm, go_hbm, tot_ref, dots_ref, codes_ref, vals_ref, pows_ref,
    dq_ref, dkv_ref,
    qbuf, gobuf, q2, go2, mbuf, deq, kv_full, sums, means, kt, s_all, dp_all,
    p_scr, ds_scr, dqbuf, acc, tx, rx, fin, sib, kvtx, kvrx, red, ag,
    in_sem, kvx_s, kvx_r, mean_s, mean_r, tx_s, rx_r, fin_r, sib_r,
    pb_s, pb_r, ag_s, ag_r,
):
    b = lax.axis_index("pb")
    ka = lax.axis_index("ka")
    z = ka // 2
    c = ka % 2
    other = 1 - c
    sibling = 2 * z + other
    inv = D ** -0.5

    barrier = pltpu.get_barrier_semaphore()
    for k in range(1, KA):
        pl.semaphore_signal(barrier, inc=1, device_id={"ka": (ka + k) % KA}, device_id_type=MESH)
    for k in range(1, PB):
        for core in range(2):
            pl.semaphore_signal(
                barrier, inc=1, device_id={"pb": (b + k) % PB, "ka": 2 * z + core}, device_id_type=MESH
            )

    q_copy = pltpu.make_async_copy(q_hbm.at[:, c], qbuf, in_sem.at[0])
    go_copy = pltpu.make_async_copy(go_hbm.at[:, c], gobuf, in_sem.at[1])
    q_copy.start()
    go_copy.start()

    both = jnp.concatenate([codes_ref[...], vals_ref[...]], axis=1)
    for h in range(2):
        row = lax.broadcasted_iota(jnp.int32, (KEYS, 2 * KEYS), 0)
        col = lax.broadcasted_iota(jnp.int32, (KEYS, 2 * KEYS), 1)
        pick = jnp.where(col == 2 * row + h, 1.0, 0.0).astype(BF16)
        picked = dot(pick, both, NN)
        total = jnp.zeros((1, D), F32)
        for blk in range(KEYS // KEYS_PER_SCALE):
            at = slice(blk * KEYS_PER_SCALE, (blk + 1) * KEYS_PER_SCALE)
            power = jnp.full((KEYS_PER_SCALE, D), pows_ref[blk, h], jnp.int32).astype(F32)
            scaled = picked[at, :D] * jnp.exp2(power)
            total = total + jnp.sum(scaled, axis=0, keepdims=True)
            deq[h, 0, at, :] = scaled.astype(BF16)
        deq[h, 1, :, :] = picked[:, D:].astype(BF16)
        sums[h] = jnp.broadcast_to(total, (8, D))

    own_rows = pl.ds(pl.multiple_of(KEYS * c, KEYS), KEYS)
    kv_full[:, own_rows, :] = deq[c]

    heads = pl.ds(pl.multiple_of(GROUP * c, GROUP), GROUP)
    pieces = split3(tot_ref[heads, :] * (D ** 0.5)) + split3(dots_ref[heads, :])
    stacked = jnp.concatenate(list(pieces) + [jnp.zeros((D - 6 * GROUP, TOK), F32)], axis=0)
    by_token = stacked.T
    lane = lax.broadcasted_iota(jnp.int32, (GROUP, D), 1)
    sub = lax.broadcasted_iota(jnp.int32, (GROUP, D), 0)
    own_lane = jnp.where((lane & (GROUP - 1)) == sub, 1.0, 0.0)
    for s in range(NZ):
        at = by_token[s * SHARE:(s + 1) * SHARE]
        spread = at[:, None, :] * own_lane[None]
        mbuf[s * ROWS:(s + 1) * ROWS, :] = spread.reshape(ROWS, D).astype(BF16)

    q_copy.wait()
    go_copy.wait()

    def flatten(s, carry):
        toks = pl.ds(s * SHARE, SHARE)
        rows = pl.ds(pl.multiple_of(s * ROWS, ROWS), ROWS)
        q2[rows, :] = qbuf[toks].astype(F32).reshape(ROWS, D).astype(BF16)
        go2[rows, :] = gobuf[toks].astype(F32).reshape(ROWS, D).astype(BF16)
        return carry

    lax.fori_loop(0, NZ, flatten, 0)

    pl.semaphore_wait(barrier, KA - 1 + 2 * (PB - 1))

    def mean_copy(k):
        peer = (ka + k) % KA
        return pltpu.make_async_remote_copy(
            src_ref=sums.at[peer % 2], dst_ref=means.at[ka], send_sem=mean_s.at[k],
            recv_sem=mean_r.at[ka], device_id={"ka": peer}, device_id_type=MESH,
        )

    def mean_arrival(k):
        peer = (ka + k) % KA
        return pltpu.make_async_remote_copy(
            src_ref=sums.at[c], dst_ref=means.at[peer], send_sem=mean_s.at[k],
            recv_sem=mean_r.at[peer], device_id={"ka": peer}, device_id_type=MESH,
        )

    swap = pltpu.make_async_remote_copy(
        src_ref=deq.at[other], dst_ref=kv_full.at[:, own_rows], send_sem=kvx_s, recv_sem=kvx_r,
        device_id={"ka": sibling}, device_id_type=MESH,
    )
    their_rows = pl.ds(pl.multiple_of(KEYS * other, KEYS), KEYS)
    swapped = pltpu.make_async_remote_copy(
        src_ref=deq.at[other], dst_ref=kv_full.at[:, their_rows], send_sem=kvx_s, recv_sem=kvx_r,
        device_id={"ka": sibling}, device_id_type=MESH,
    )
    for k in range(1, KA):
        mean_copy(k).start()
    swap.start()
    swapped.wait_recv()

    lanes = lax.broadcasted_iota(jnp.int32, (CKEYS, D), 1)
    k_ones = jnp.where(lanes < 3 * GROUP, -1.0, 0.0).astype(BF16)
    v_ones = jnp.where((lanes >= 3 * GROUP) & (lanes < 6 * GROUP), -1.0, 0.0).astype(BF16)

    def first(s, carry):
        rows = pl.ds(pl.multiple_of(s * ROWS, ROWS), ROWS)
        extra = mbuf[rows, :]
        k_in = jnp.concatenate([kv_full[0], k_ones], axis=1)
        v_in = jnp.concatenate([kv_full[1], v_ones], axis=1)
        s_all[s] = dot(k_in, jnp.concatenate([q2[rows, :], extra], axis=1), NT)
        dp_all[s] = dot(v_in, jnp.concatenate([go2[rows, :], extra], axis=1), NT)
        return carry

    lax.fori_loop(0, NZ, first, 0)

    for k in range(1, KA):
        mean_arrival(k).wait_recv()
    means[ka] = sums[c]
    mean = jnp.sum(means[...], axis=0) / (KA * KEYS)
    smoothed = kv_full[0].astype(F32) - mean[0:1]
    kt[...] = smoothed.T.astype(BF16)
    m_hi, m_mid, m_lo = split3(mean)
    srow = lax.broadcasted_iota(jnp.int32, (8, D), 0)
    mean_rows = jnp.where(srow == 0, m_hi, jnp.where(srow == 1, m_mid, jnp.where(srow == 2, m_lo, 0.0)))
    mean_rows = jnp.concatenate([mean_rows, jnp.zeros((8, D), F32)], axis=0).astype(BF16)
    acc[...] = jnp.zeros_like(acc)

    def offset(t):
        return jnp.where(t % 2 == 1, (t - 1) // 2 - 3, NZ // 2 - t // 2)

    left = (z + NZ - 1) % NZ
    right = (z + 1) % NZ

    def hop(t, half):
        leftward = half == 0 if t == 0 else t % 2 == 1
        to = left if leftward else right
        if t < 5:
            at = (1 if half == 0 else 2) if t == 0 else t + 2
            return pltpu.make_async_remote_copy(
                src_ref=tx.at[t, half], dst_ref=rx.at[at, half], send_sem=tx_s.at[t, half],
                recv_sem=rx_r.at[at, half], device_id={"ka": 2 * to + c}, device_id_type=MESH,
            )
        side = 0 if leftward else 1
        return pltpu.make_async_remote_copy(
            src_ref=tx.at[t, half], dst_ref=fin.at[side, c], send_sem=tx_s.at[t, half],
            recv_sem=fin_r.at[side, c], device_id={"ka": 2 * to + half}, device_id_type=MESH,
        )

    def arrival(t, half):
        return pltpu.make_async_remote_copy(
            src_ref=tx.at[t, half], dst_ref=rx.at[t, half], send_sem=tx_s.at[t, half],
            recv_sem=rx_r.at[t, half], device_id={"ka": sibling}, device_id_type=MESH,
        )

    def part(t, half):
        return dqbuf[t, half * HALF:(half + 1) * HALF, :]

    def begin(t, half):
        tx[t, half] = part(t, half).astype(BF16)
        hop(t, half).start()

    def forward(t, half):
        arrival(t, half).wait_recv()
        tx[t, half] = (part(t, half) + rx[t, half].astype(F32)).astype(BF16)
        hop(t, half).start()

    def second(t, carry):
        s = (z + offset(t) + NZ) % NZ
        rows = pl.ds(pl.multiple_of(s * ROWS, ROWS), ROWS)
        q_in = q2[rows, :]
        go_in = go2[rows, :]
        shift = jnp.sum(dot(mean_rows, q_in, NT)[0:8], axis=0, keepdims=True)
        limit = TOK * b + SHARE * s - CKEYS * z
        token = lax.shift_right_logical(lax.broadcasted_iota(jnp.int32, (16, ROWS), 1), 3)
        gap = lax.broadcasted_iota(jnp.int32, (16, ROWS), 0) - token
        for k0 in range(0, CKEYS, 16):
            scores = (s_all[s, k0:k0 + 16, :] - shift) * (inv * LOG2E)
            w = jnp.where(gap + k0 <= limit, jnp.exp2(scores), 0.0)
            p_scr[k0:k0 + 16, :] = w.astype(BF16)
            ds_scr[k0:k0 + 16, :] = (w * dp_all[s, k0:k0 + 16, :]).astype(BF16)
        p_in = p_scr[...]
        ds_in = ds_scr[...]
        dqbuf[t] = (dot(kt[...], ds_in, NN) * inv).T
        acc[0] += dot(ds_in, q_in, NN)
        acc[1] += dot(p_in, go_in, NN)

        @pl.when(t == 0)
        def _():
            begin(0, 0)
            begin(0, 1)

        @pl.when(t == 1)
        def _():
            begin(1, 1)

        @pl.when(t == 2)
        def _():
            begin(2, 0)

        @pl.when(t == 4)
        def _():
            forward(1, 0)
            forward(2, 1)

        return carry

    lax.fori_loop(0, NZ, second, 0)

    kvtx[0] = (acc[0] * inv).astype(BF16)
    kvtx[1] = acc[1].astype(BF16)

    def piece_copy(k):
        peer = (b + k) % PB
        return pltpu.make_async_remote_copy(
            src_ref=kvtx.at[:, pl.ds(pl.multiple_of(peer * PIECE, PIECE), PIECE)], dst_ref=kvrx.at[b],
            send_sem=pb_s.at[k], recv_sem=pb_r.at[b], device_id={"pb": peer}, device_id_type=MESH,
        )

    def piece_arrival(k):
        peer = (b + k) % PB
        return pltpu.make_async_remote_copy(
            src_ref=kvtx.at[:, pl.ds(pl.multiple_of(peer * PIECE, PIECE), PIECE)], dst_ref=kvrx.at[peer],
            send_sem=pb_s.at[k], recv_sem=pb_r.at[peer], device_id={"pb": peer}, device_id_type=MESH,
        )

    for k in range(1, PB):
        piece_copy(k).start()

    tx[7, 0] = part(7, 0).astype(BF16)
    tx[7, 1] = part(7, 1).astype(BF16)
    to_sib = pltpu.make_async_remote_copy(
        src_ref=tx.at[7, other], dst_ref=sib, send_sem=tx_s.at[7, 0], recv_sem=sib_r,
        device_id={"ka": sibling}, device_id_type=MESH,
    )
    to_sib.start()

    for t in (3, 4, 5, 6):
        for half in range(2):
            forward(t, half)

    for k in range(1, PB):
        piece_arrival(k).wait_recv()
    kvrx[b] = kvtx[:, pl.ds(pl.multiple_of(b * PIECE, PIECE), PIECE), :]
    gathered = kvrx[0].astype(F32)
    for k in range(1, PB):
        gathered = gathered + kvrx[k].astype(F32)
    red[...] = gathered.astype(BF16)

    owner = b // (PB // 2)
    slot = b % (PB // 2)
    goal = ag.at[:, c, pl.ds(pl.multiple_of(slot * PIECE, PIECE), PIECE)]

    def spread_copy(k):
        return pltpu.make_async_remote_copy(
            src_ref=red, dst_ref=goal, send_sem=ag_s.at[k], recv_sem=ag_r.at[c, slot],
            device_id={"pb": (b + k) % PB, "ka": 2 * z + owner}, device_id_type=MESH,
        )

    def spread_arrival(h, sl):
        return pltpu.make_async_remote_copy(
            src_ref=red, dst_ref=ag.at[:, h, pl.ds(sl * PIECE, PIECE)], send_sem=ag_s.at[0],
            recv_sem=ag_r.at[h, sl], device_id={"ka": sibling}, device_id_type=MESH,
        )

    for k in range(1, PB):
        spread_copy(k).start()

    @pl.when(owner == c)
    def _():
        ag[:, c, pl.ds(pl.multiple_of(slot * PIECE, PIECE), PIECE), :] = red[...]

    @pl.when(owner != c)
    def _():
        spread_copy(0).start()

    for side in range(2):
        for h in range(2):
            pltpu.make_async_remote_copy(
                src_ref=tx.at[5, 0], dst_ref=fin.at[side, h], send_sem=tx_s.at[5, 0],
                recv_sem=fin_r.at[side, h], device_id={"ka": sibling}, device_id_type=MESH,
            ).wait_recv()
    to_sib.wait_recv()
    mine = dqbuf[7, pl.ds(pl.multiple_of(c * HALF, HALF), HALF), :]
    for h, local in ((c, mine), (other, sib[...].astype(F32))):
        whole = local + fin[0, h].astype(F32) + fin[1, h].astype(F32)
        dq_ref[:, h] = whole.reshape(HALF // GROUP, GROUP, D).astype(BF16)

    for h in range(2):
        for sl in range(PB // 2):
            @pl.when(jnp.logical_not((owner == c) & (slot == sl) & (c == h)))
            def _():
                spread_arrival(h, sl).wait_recv()
    dkv_ref[...] = ag[...]

    for k in range(1, KA):
        mean_copy(k).wait_send()
    swap.wait_send()
    for t in range(7):
        for half in range(2):
            hop(t, half).wait_send()
    to_sib.wait_send()
    for k in range(1, PB):
        piece_copy(k).wait_send()
        spread_copy(k).wait_send()

    @pl.when(owner != c)
    def _():
        spread_copy(0).wait_send()


def per_device(queries, key_codes, key_scale_powers, values, grad_out, grad_dot, log_totals):
    vmem = pl.BlockSpec(memory_space=pltpu.VMEM)
    anyw = pl.BlockSpec(memory_space=pl.ANY)
    dma = pltpu.SemaphoreType.DMA
    dq, dkv = pl.pallas_call(
        kernel,
        out_shape=(
            jax.ShapeDtypeStruct((TOK // KA, 2, GROUP, D), BF16),
            jax.ShapeDtypeStruct((2, 2, KEYS, D), BF16),
        ),
        in_specs=[anyw, anyw, vmem, vmem, vmem, vmem, pl.BlockSpec(memory_space=pltpu.SMEM)],
        out_specs=(vmem, vmem),
        scratch_shapes=[
            pltpu.VMEM((TOK, GROUP, D), BF16),
            pltpu.VMEM((TOK, GROUP, D), BF16),
            pltpu.VMEM((TOK * GROUP, D), BF16),
            pltpu.VMEM((TOK * GROUP, D), BF16),
            pltpu.VMEM((TOK * GROUP, D), BF16),
            pltpu.VMEM((2, 2, KEYS, D), BF16),
            pltpu.VMEM((2, CKEYS, D), BF16),
            pltpu.VMEM((2, 8, D), F32),
            pltpu.VMEM((KA, 8, D), F32),
            pltpu.VMEM((D, CKEYS), BF16),
            pltpu.VMEM((NZ, CKEYS, ROWS), F32),
            pltpu.VMEM((NZ, CKEYS, ROWS), F32),
            pltpu.VMEM((CKEYS, ROWS), BF16),
            pltpu.VMEM((CKEYS, ROWS), BF16),
            pltpu.VMEM((NZ, ROWS, D), F32),
            pltpu.VMEM((2, CKEYS, D), F32),
            pltpu.VMEM((NZ, 2, HALF, D), BF16),
            pltpu.VMEM((7, 2, HALF, D), BF16),
            pltpu.VMEM((2, 2, HALF, D), BF16),
            pltpu.VMEM((HALF, D), BF16),
            pltpu.VMEM((2, CKEYS, D), BF16),
            pltpu.VMEM((PB, 2, PIECE, D), BF16),
            pltpu.VMEM((2, PIECE, D), BF16),
            pltpu.VMEM((2, 2, KEYS, D), BF16),
            dma((2,)),
            dma,
            dma,
            dma((KA,)),
            dma((KA,)),
            dma((NZ, 2)),
            dma((7, 2)),
            dma((2, 2)),
            dma,
            dma((PB,)),
            dma((PB,)),
            dma((PB,)),
            dma((2, PB // 2)),
        ],
        compiler_params=pltpu.CompilerParams(collective_id=0, has_side_effects=True),
    )(
        queries.reshape(TOK, 2, GROUP, D),
        grad_out.reshape(TOK, 2, GROUP, D),
        log_totals.T,
        grad_dot.T,
        key_codes.reshape(2 * KEYS, D),
        values.reshape(2 * KEYS, D),
        key_scale_powers,
    )
    return (
        dq.reshape(TOK // KA, 2 * GROUP, D),
        jnp.swapaxes(dkv[0], 0, 1),
        jnp.swapaxes(dkv[1], 0, 1),
    )


def solution(mesh):
    in_specs = (
        P("pb", "ha", None),
        P("ka", "ha", None),
        P("ka", "ha"),
        P("ka", "ha", None),
        P("pb", "ha", None),
        P("pb", "ha"),
        P("pb", "ha"),
    )
    out_specs = (P(("pb", "ka"), "ha", None), P("ka", "ha", None), P("ka", "ha", None))
    return jax.shard_map(
        per_device, mesh=mesh, in_specs=in_specs, out_specs=out_specs, check_vma=False
    )
```

time: 106 us -> 43.7 us (0.41)
  waiting for transfers between devices: 55.4 us -> 0 us
  Pallas kernels: 0 us -> 37.5 us
  starting transfers between devices: 25.5 us -> 0 us
  matrix products: 7.85 us -> 0 us
  local copies, waits for them, and re-layouts: 12 us -> 5.32 us
  other arithmetic: 3.38 us -> 0 us
    all_to_all x4 -> x0, waiting for transfers between devices: 55.4 us -> none  [the longest x1 36.9 us: sum_at_owner(): lax.all_to_all(pieces, axis, split_axis=0, concat_axis=0, tiled=True)]
    pallas_call x0 -> x1, Pallas kernels: none -> 37.5 us  [per_device(): pl.pallas_call(kernel, out_shape=(jax.ShapeDtypeStruct((TOK // KA, 2, GRO...]
    all_to_all x4 -> x0, starting transfers between devices: 25.5 us -> none  [the longest x3 20.8 us: copy_for_each(): lax.all_to_all(jnp.broadcast_to(array[None], (peers, *array.shape)), axis...]
    dot_general x10 -> x0, matrix products: 7.85 us -> none  [the longest x2 3.87 us: head_grads(): jnp.einsum('igd,jd->gij', grad_block, value_block, preferred_element_type...]
    slice x3 -> x0, local copies, waits for them, and re-layouts: 2.86 us -> none  [the longest x1 1.48 us: per_device(): query_in[query_range, chosen]]
    broadcast_in_dim x4 -> x0, local copies, waits for them, and re-layouts: 2.77 us -> none  [the longest x3 2.7 us: copy_for_each(): jnp.broadcast_to(array[None], (peers, *array.shape))]
    reduce_sum x5 -> x0, other arithmetic: 2.14 us -> none  [the longest x1 1.02 us: per_device(): key_total = over_copies(jnp.sum(dequantized, axis=0), 'ka')]
    concatenate x1 -> x0, local copies, waits for them, and re-layouts: 2.01 us -> none  [per_device(): grad_query = jnp.concatenate(query_parts, axis=1)]
  transfers between devices with their start and end apart: 4 -> 0, of which waited for: 4 -> 0; matrix products, arithmetic and copies ran while one was open for 12% -> 0% of each run, Pallas kernels for 0% -> 0%
where the time goes in v1:
time: 43.7 us; the launch traced here: 43.5 us
  Pallas kernels  37.5 us (86%)
  local copies, waits for them, and re-layouts  5.32 us (12%)
  between operations  0.64 us (1%)
    pallas_call x1, Pallas kernels, per_device(): pl.pallas_call(kernel, out_shape=(jax.ShapeDtypeStruct((TOK // KA, 2, GRO...  37.5 us
    unnamed x4, local copies, waits for them, and re-layouts  4.36 us
    transpose x1, local copies, waits for them, and re-layouts, per_device(): jnp.swapaxes(dkv[1], 0, 1)  0.96 us

profile of v1, /device:TPU:1, one launch (start us, length us, event | category | flops | bytes accessed | tf_op | source)
XLA Modules:
  0.0 43.5 jit_solution(9085977485679982464)
XLA Ops:
  0.6 1.3 %copy.10.pows_ref = s32[3,2]{1,0:T(4,128)} copy(s32[3,2]{0,1:T(2,128)} %param.9) | data formatting | bytes 48 | tf_op args[2]
  2.0 37.5 %shard_map.94 = (bf16[24,2,8,128]{3,2,1,0:T(8,128)(2,1)}, bf16[2,2,192,128]{3,2,1,0:T(8,128)(2,1)}) custom-call(bf16[384,2,8,128]{3,2,1,0:T(8,128)(2,1)} %bitcast.15, bf16[384,2,8,128]{3,2,1,0:T(8,128)(2,1)} %bitcast.16, f32[16,384]{1,0:T(8,128)} %bitcast.20, f32[16,384]{1,0:T(8,128)} %bitcast.21, bf16[384,128]{1,0:T(8,128)(2,1)} %bitcast.17, ...), custom_call_target="tpu_custom_call" | custom-call | tf_op jit(solution)/shard_map/pallas_call | solution.py:360
  39.5 1.0 %slice_bitcast_fusion = (bf16[192,2,128]{2,0,1:T(8,128)(2,1)S(1)}, bf16[192,2,128]{2,0,1:T(8,128)(2,1)S(1)}) fusion(bf16[2,2,192,128]{3,2,1,0:T(8,128)(2,1)} %get-tuple-element.6), kind=kLoop, calls=%fused_computation | loop fusion | bytes 393216 | tf_op jit(solution)/shard_map/transpose | solution.py:420
  40.5 0.7 %copy.12 = bf16[192,2,128]{2,1,0:T(2,128)(2,1)} copy(bf16[192,2,128]{2,0,1:T(8,128)(2,1)S(1)} %get-tuple-element.10) | data formatting | bytes 196608
  41.2 0.7 %copy.11 = bf16[192,2,128]{2,1,0:T(2,128)(2,1)} copy(bf16[192,2,128]{2,0,1:T(8,128)(2,1)S(1)} %get-tuple-element.11) | data formatting | bytes 196608
  41.9 1.5 %copy.14 = bf16[24,16,128]{2,1,0:T(8,128)(2,1)} copy(bf16[24,16,128]{2,1,0:T(8,128)(2,1)} %bitcast.19) | data formatting | bytes 196608

commit v2 on v1

--- a/solution.py
+++ b/solution.py
@@ -27,6 +27,8 @@
 PIECE = CKEYS // PB
 KEYS_PER_SCALE = 64
 LOG2E = 1.4426950408889634
+HIDDEN = -1e30
+FAR_FIRST = sorted(range(1, KA), key=lambda k: (abs(k - KA // 2), k))
 
 
 def dot(a, b, dims):
@@ -41,10 +43,11 @@
 
 
 def kernel(
-    q_hbm, go_hbm, tot_ref, dots_ref, codes_ref, vals_ref, pows_ref,
+    q_hbm, go_hbm, tot_hbm, dots_hbm, codes_hbm, vals_hbm, pows_hbm,
     dq_ref, dkv_ref,
+    tot_ref, dots_ref, codes_ref, vals_ref, pows_ref, merge,
     qbuf, gobuf, q2, go2, mbuf, deq, kv_full, sums, means, kt, s_all, dp_all,
-    p_scr, ds_scr, dqbuf, acc, tx, rx, fin, sib, kvtx, kvrx, red, ag,
+    stab, totf, gain, dqt, p_scr, ds_scr, dqbuf, acc, tx, rx, fin, sib, kvtx, kvrx, red, ag,
     in_sem, kvx_s, kvx_r, mean_s, mean_r, tx_s, rx_r, fin_r, sib_r,
     pb_s, pb_r, ag_s, ag_r,
 ):
@@ -57,7 +60,7 @@
     inv = D ** -0.5
 
     barrier = pltpu.get_barrier_semaphore()
-    for k in range(1, KA):
+    for k in FAR_FIRST:
         pl.semaphore_signal(barrier, inc=1, device_id={"ka": (ka + k) % KA}, device_id_type=MESH)
     for k in range(1, PB):
         for core in range(2):
@@ -67,8 +70,20 @@
 
     q_copy = pltpu.make_async_copy(q_hbm.at[:, c], qbuf, in_sem.at[0])
     go_copy = pltpu.make_async_copy(go_hbm.at[:, c], gobuf, in_sem.at[1])
+    heads = pl.ds(pl.multiple_of(GROUP * c, GROUP), GROUP)
+    loads = [
+        pltpu.make_async_copy(codes_hbm, codes_ref, in_sem.at[2]),
+        pltpu.make_async_copy(vals_hbm, vals_ref, in_sem.at[3]),
+        pltpu.make_async_copy(pows_hbm, pows_ref, in_sem.at[4]),
+        pltpu.make_async_copy(tot_hbm.at[heads], tot_ref, in_sem.at[5]),
+        pltpu.make_async_copy(dots_hbm.at[heads], dots_ref, in_sem.at[6]),
+    ]
+    for load in loads:
+        load.start()
     q_copy.start()
     go_copy.start()
+    for load in loads:
+        load.wait()
 
     both = jnp.concatenate([codes_ref[...], vals_ref[...]], axis=1)
     for h in range(2):
@@ -79,18 +94,17 @@
         total = jnp.zeros((1, D), F32)
         for blk in range(KEYS // KEYS_PER_SCALE):
             at = slice(blk * KEYS_PER_SCALE, (blk + 1) * KEYS_PER_SCALE)
-            power = jnp.full((KEYS_PER_SCALE, D), pows_ref[blk, h], jnp.int32).astype(F32)
+            power = jnp.full((KEYS_PER_SCALE, D), pows_ref[h, blk], jnp.int32).astype(F32)
             scaled = picked[at, :D] * jnp.exp2(power)
             total = total + jnp.sum(scaled, axis=0, keepdims=True)
             deq[h, 0, at, :] = scaled.astype(BF16)
         deq[h, 1, :, :] = picked[:, D:].astype(BF16)
-        sums[h] = jnp.broadcast_to(total, (8, D))
+        sums[h] = total
 
     own_rows = pl.ds(pl.multiple_of(KEYS * c, KEYS), KEYS)
     kv_full[:, own_rows, :] = deq[c]
 
-    heads = pl.ds(pl.multiple_of(GROUP * c, GROUP), GROUP)
-    pieces = split3(tot_ref[heads, :] * (D ** 0.5)) + split3(dots_ref[heads, :])
+    pieces = split3(tot_ref[...] * (D ** 0.5)) + split3(dots_ref[...])
     stacked = jnp.concatenate(list(pieces) + [jnp.zeros((D - 6 * GROUP, TOK), F32)], axis=0)
     by_token = stacked.T
     lane = lax.broadcasted_iota(jnp.int32, (GROUP, D), 1)
@@ -138,7 +152,7 @@
         src_ref=deq.at[other], dst_ref=kv_full.at[:, their_rows], send_sem=kvx_s, recv_sem=kvx_r,
         device_id={"ka": sibling}, device_id_type=MESH,
     )
-    for k in range(1, KA):
+    for k in FAR_FIRST:
         mean_copy(k).start()
     swap.start()
     swapped.wait_recv()
@@ -147,23 +161,58 @@
     k_ones = jnp.where(lanes < 3 * GROUP, -1.0, 0.0).astype(BF16)
     v_ones = jnp.where((lanes >= 3 * GROUP) & (lanes < 6 * GROUP), -1.0, 0.0).astype(BF16)
 
-    def first(s, carry):
-        rows = pl.ds(pl.multiple_of(s * ROWS, ROWS), ROWS)
-        extra = mbuf[rows, :]
-        k_in = jnp.concatenate([kv_full[0], k_ones], axis=1)
-        v_in = jnp.concatenate([kv_full[1], v_ones], axis=1)
-        s_all[s] = dot(k_in, jnp.concatenate([q2[rows, :], extra], axis=1), NT)
-        dp_all[s] = dot(v_in, jnp.concatenate([go2[rows, :], extra], axis=1), NT)
+    kt[0:D, :] = kv_full[0].astype(F32).T.astype(BF16)
+    kt[D:, :] = jnp.ones((16, CKEYS), BF16)
+    token = lax.shift_right_logical(lax.broadcasted_iota(jnp.int32, (16, ROWS), 1), 3)
+    gap = lax.broadcasted_iota(jnp.int32, (16, ROWS), 0) - token
+
+    def first(i, carry):
+        places = []
+        for at in range(2):
+            s = 2 * i + at
+            places.append((at, s, pl.ds(pl.multiple_of(s * ROWS, ROWS), ROWS)))
+        for at, s, rows in places:
+            extra = mbuf[rows, :]
+            k_in = jnp.concatenate([kv_full[0], k_ones], axis=1)
+            v_in = jnp.concatenate([kv_full[1], v_ones], axis=1)
+            s_all[s] = dot(k_in, jnp.concatenate([q2[rows, :], extra], axis=1), NT)
+            dp_all[s] = dot(v_in, jnp.concatenate([go2[rows, :], extra], axis=1), NT)
+        for at, s, rows in places:
+            limit = TOK * b + SHARE * s - CKEYS * z
+            top = jnp.full((16, ROWS), HIDDEN, F32)
+            for k0 in range(0, CKEYS, 16):
+                a = jnp.where(gap + k0 <= limit, s_all[s, k0:k0 + 16, :] * (inv * LOG2E), HIDDEN)
+                s_all[s, k0:k0 + 16, :] = a
+                top = jnp.maximum(top, a)
+            peak = jnp.max(top, axis=0, keepdims=True)
+            stab[s] = peak
+            for k0 in range(0, CKEYS, 16):
+                w = jnp.exp2(s_all[s, k0:k0 + 16, :] - peak)
+                f = w * dp_all[s, k0:k0 + 16, :]
+                s_all[s, k0:k0 + 16, :] = w
+                dp_all[s, k0:k0 + 16, :] = f
+                ds_scr[at, k0:k0 + 16, :] = f.astype(BF16)
+        for at, s, rows in places:
+            both_sums = dot(kt[...], ds_scr[at], NN)
+            dqt[s] = both_sums[0:D]
+            totf[s] = both_sums[D:D + 1]
         return carry
 
-    lax.fori_loop(0, NZ, first, 0)
+    lax.fori_loop(0, NZ // 2, first, 0)
+
+    m_row = lax.broadcasted_iota(jnp.int32, (2 * KEYS, KEYS), 0)
+    m_col = lax.broadcasted_iota(jnp.int32, (2 * KEYS, KEYS), 1)
+    for h in range(2):
+        merge[h] = jnp.where(m_row == 2 * m_col + h, 1.0, 0.0).astype(BF16)
 
     for k in range(1, KA):
         mean_arrival(k).wait_recv()
     means[ka] = sums[c]
-    mean = jnp.sum(means[...], axis=0) / (KA * KEYS)
-    smoothed = kv_full[0].astype(F32) - mean[0:1]
-    kt[...] = smoothed.T.astype(BF16)
+    total = means[0]
+    for k in range(1, KA):
+        total = total + means[k]
+    mean = jnp.broadcast_to(total / (KA * KEYS), (8, D))
+    mean_col = jnp.broadcast_to(mean[0:1], (D, D)).T
     m_hi, m_mid, m_lo = split3(mean)
     srow = lax.broadcasted_iota(jnp.int32, (8, D), 0)
     mean_rows = jnp.where(srow == 0, m_hi, jnp.where(srow == 1, m_mid, jnp.where(srow == 2, m_lo, 0.0)))
@@ -209,47 +258,46 @@
         tx[t, half] = (part(t, half) + rx[t, half].astype(F32)).astype(BF16)
         hop(t, half).start()
 
-    def second(t, carry):
+    def finish_share(t):
         s = (z + offset(t) + NZ) % NZ
         rows = pl.ds(pl.multiple_of(s * ROWS, ROWS), ROWS)
-        q_in = q2[rows, :]
-        go_in = go2[rows, :]
-        shift = jnp.sum(dot(mean_rows, q_in, NT)[0:8], axis=0, keepdims=True)
-        limit = TOK * b + SHARE * s - CKEYS * z
-        token = lax.shift_right_logical(lax.broadcasted_iota(jnp.int32, (16, ROWS), 1), 3)
-        gap = lax.broadcasted_iota(jnp.int32, (16, ROWS), 0) - token
-        for k0 in range(0, CKEYS, 16):
-            scores = (s_all[s, k0:k0 + 16, :] - shift) * (inv * LOG2E)
-            w = jnp.where(gap + k0 <= limit, jnp.exp2(scores), 0.0)
-            p_scr[k0:k0 + 16, :] = w.astype(BF16)
-            ds_scr[k0:k0 + 16, :] = (w * dp_all[s, k0:k0 + 16, :]).astype(BF16)
-        p_in = p_scr[...]
-        ds_in = ds_scr[...]
-        dqbuf[t] = (dot(kt[...], ds_in, NN) * inv).T
-        acc[0] += dot(ds_in, q_in, NN)
-        acc[1] += dot(p_in, go_in, NN)
-
-        @pl.when(t == 0)
-        def _():
+        shift = jnp.sum(dot(mean_rows, q2[rows, :], NT)[0:8], axis=0, keepdims=True)
+        factor = jnp.exp2(stab[s] - shift * (inv * LOG2E))
+        gain[s] = factor
+        for l0 in range(0, ROWS, D):
+            at = slice(l0, l0 + D)
+            centred = dqt[s, :, at] - mean_col * totf[s, :, at]
+            dqbuf[t, at, :] = (centred * (factor[:, at] * inv)).T
+
+    for t in range(NZ):
+        finish_share(t)
+        if t == 0:
             begin(0, 0)
             begin(0, 1)
-
-        @pl.when(t == 1)
-        def _():
+        elif t == 1:
             begin(1, 1)
-
-        @pl.when(t == 2)
-        def _():
+        elif t == 2:
             begin(2, 0)
 
-        @pl.when(t == 4)
-        def _():
-            forward(1, 0)
-            forward(2, 1)
-
+    def second(i, carry):
+        places = []
+        for at in range(2):
+            s = 2 * i + at
+            places.append((at, s, pl.ds(pl.multiple_of(s * ROWS, ROWS), ROWS)))
+        for at, s, rows in places:
+            factor = gain[s]
+            for k0 in range(0, CKEYS, 16):
+                p_scr[at, k0:k0 + 16, :] = (s_all[s, k0:k0 + 16, :] * factor).astype(BF16)
+                ds_scr[at, k0:k0 + 16, :] = (dp_all[s, k0:k0 + 16, :] * factor).astype(BF16)
+        add_k, add_v = acc[0], acc[1]
+        for at, s, rows in places:
+            add_k = add_k + dot(ds_scr[at], q2[rows, :], NN)
+            add_v = add_v + dot(p_scr[at], go2[rows, :], NN)
+        acc[0] = add_k
+        acc[1] = add_v
         return carry
 
-    lax.fori_loop(0, NZ, second, 0)
+    lax.fori_loop(0, NZ // 2, second, 0)
 
     kvtx[0] = (acc[0] * inv).astype(BF16)
     kvtx[1] = acc[1].astype(BF16)
@@ -279,6 +327,8 @@
     )
     to_sib.start()
 
+    forward(1, 0)
+    forward(2, 1)
     for t in (3, 4, 5, 6):
         for half in range(2):
             forward(t, half)
@@ -335,7 +385,10 @@
             @pl.when(jnp.logical_not((owner == c) & (slot == sl) & (c == h)))
             def _():
                 spread_arrival(h, sl).wait_recv()
-    dkv_ref[...] = ag[...]
+    side_by_side = [jnp.concatenate([ag[0, h], ag[1, h]], axis=1) for h in range(2)]
+    merged = dot(merge[0], side_by_side[0], NN) + dot(merge[1], side_by_side[1], NN)
+    dkv_ref[0] = merged[:, :D].astype(BF16)
+    dkv_ref[1] = merged[:, D:].astype(BF16)
 
     for k in range(1, KA):
         mean_copy(k).wait_send()
@@ -353,6 +406,18 @@
         spread_copy(0).wait_send()
 
 
+def write_out(dq_ref, dkv_ref, dq_hbm, dk_hbm, dv_hbm, sems):
+    copies = [
+        pltpu.make_async_copy(dq_ref, dq_hbm, sems.at[0]),
+        pltpu.make_async_copy(dkv_ref.at[0], dk_hbm, sems.at[1]),
+        pltpu.make_async_copy(dkv_ref.at[1], dv_hbm, sems.at[2]),
+    ]
+    for copy in copies:
+        copy.start()
+    for copy in copies:
+        copy.wait()
+
+
 def per_device(queries, key_codes, key_scale_powers, values, grad_out, grad_dot, log_totals):
     vmem = pl.BlockSpec(memory_space=pltpu.VMEM)
     anyw = pl.BlockSpec(memory_space=pl.ANY)
@@ -360,12 +425,18 @@
     dq, dkv = pl.pallas_call(
         kernel,
         out_shape=(
-            jax.ShapeDtypeStruct((TOK // KA, 2, GROUP, D), BF16),
-            jax.ShapeDtypeStruct((2, 2, KEYS, D), BF16),
+            pltpu.VMEM((TOK // KA, 2, GROUP, D), BF16),
+            pltpu.VMEM((2, 2 * KEYS, D), BF16),
         ),
-        in_specs=[anyw, anyw, vmem, vmem, vmem, vmem, pl.BlockSpec(memory_space=pltpu.SMEM)],
+        in_specs=[anyw] * 7,
         out_specs=(vmem, vmem),
         scratch_shapes=[
+            pltpu.VMEM((GROUP, TOK), F32),
+            pltpu.VMEM((GROUP, TOK), F32),
+            pltpu.VMEM((2 * KEYS, D), BF16),
+            pltpu.VMEM((2 * KEYS, D), BF16),
+            pltpu.SMEM((2, KEYS // KEYS_PER_SCALE), jnp.int32),
+            pltpu.VMEM((2, 2 * KEYS, KEYS), BF16),
             pltpu.VMEM((TOK, GROUP, D), BF16),
             pltpu.VMEM((TOK, GROUP, D), BF16),
             pltpu.VMEM((TOK * GROUP, D), BF16),
@@ -373,13 +444,17 @@
             pltpu.VMEM((TOK * GROUP, D), BF16),
             pltpu.VMEM((2, 2, KEYS, D), BF16),
             pltpu.VMEM((2, CKEYS, D), BF16),
-            pltpu.VMEM((2, 8, D), F32),
-            pltpu.VMEM((KA, 8, D), F32),
-            pltpu.VMEM((D, CKEYS), BF16),
+            pltpu.VMEM((2, 1, D), F32),
+            pltpu.VMEM((KA, 1, D), F32),
+            pltpu.VMEM((D + 16, CKEYS), BF16),
             pltpu.VMEM((NZ, CKEYS, ROWS), F32),
             pltpu.VMEM((NZ, CKEYS, ROWS), F32),
-            pltpu.VMEM((CKEYS, ROWS), BF16),
-            pltpu.VMEM((CKEYS, ROWS), BF16),
+            pltpu.VMEM((NZ, 1, ROWS), F32),
+            pltpu.VMEM((NZ, 1, ROWS), F32),
+            pltpu.VMEM((NZ, 1, ROWS), F32),
+            pltpu.VMEM((NZ, D, ROWS), F32),
+            pltpu.VMEM((2, CKEYS, ROWS), BF16),
+            pltpu.VMEM((2, CKEYS, ROWS), BF16),
             pltpu.VMEM((NZ, ROWS, D), F32),
             pltpu.VMEM((2, CKEYS, D), F32),
             pltpu.VMEM((NZ, 2, HALF, D), BF16),
@@ -390,7 +465,7 @@
             pltpu.VMEM((PB, 2, PIECE, D), BF16),
             pltpu.VMEM((2, PIECE, D), BF16),
             pltpu.VMEM((2, 2, KEYS, D), BF16),
-            dma((2,)),
+            dma((7,)),
             dma,
             dma,
             dma((KA,)),
@@ -412,12 +487,24 @@
         grad_dot.T,
         key_codes.reshape(2 * KEYS, D),
         values.reshape(2 * KEYS, D),
-        key_scale_powers,
-    )
+        key_scale_powers.T,
+    )
+    dq, dk, dv = pl.pallas_call(
+        write_out,
+        out_shape=(
+            jax.ShapeDtypeStruct((TOK // KA, 2, GROUP, D), BF16),
+            jax.ShapeDtypeStruct((2 * KEYS, D), BF16),
+            jax.ShapeDtypeStruct((2 * KEYS, D), BF16),
+        ),
+        in_specs=[vmem, vmem],
+        out_specs=(anyw, anyw, anyw),
+        scratch_shapes=[dma((3,))],
+        compiler_params=pltpu.CompilerParams(vmem_limit_bytes=4 * 1024 * 1024),
+    )(dq, dkv)
     return (
         dq.reshape(TOK // KA, 2 * GROUP, D),
-        jnp.swapaxes(dkv[0], 0, 1),
-        jnp.swapaxes(dkv[1], 0, 1),
+        dk.reshape(KEYS, 2, D),
+        dv.reshape(KEYS, 2, D),
     )
 
 

time: 43.7 us -> 36.4 us (0.83)
  local copies, waits for them, and re-layouts: 5.32 us -> 0 us
  Pallas kernels: 37.5 us -> 35.6 us
    unnamed x4 -> x0, local copies, waits for them, and re-layouts: 4.36 us -> none
    pallas_call x1 -> x2, Pallas kernels: 37.5 us -> 35.6 us  [the longest x1 34.9 us: per_device(): pl.pallas_call(kernel, out_shape=(pltpu.VMEM((TOK // KA, 2, GROUP, D), BF...]
    transpose x1 -> x0, local copies, waits for them, and re-layouts: 0.96 us -> none  [per_device(): jnp.swapaxes(dkv[1], 0, 1)]
where the time goes in v2:
time: 36.4 us; the launch traced here: 36.3 us
  Pallas kernels  35.6 us (98%)
  between operations  0.64 us (2%)
    pallas_call x1, Pallas kernels, per_device(): pl.pallas_call(kernel, out_shape=(pltpu.VMEM((TOK // KA, 2, GROUP, D), BF...  34.9 us
    pallas_call x1, Pallas kernels, per_device(): pl.pallas_call(write_out, out_shape=(jax.ShapeDtypeStruct((TOK // KA, 2,...  0.73 us

profile of v2, /device:TPU:1, one launch (start us, length us, event | category | flops | bytes accessed | tf_op | source)
XLA Modules:
  0.0 36.3 jit_solution(6793030748866014974)
XLA Ops:
  0.6 34.9 %shard_map.94 = (bf16[24,2,8,128]{3,2,1,0:T(8,128)(2,1)S(1)}, bf16[2,384,128]{2,1,0:T(8,128)(2,1)S(1)}) custom-call(bf16[384,2,8,128]{3,2,1,0:T(8,128)(2,1)} %bitcast.10, bf16[384,2,8,128]{3,2,1,0:T(8,128)(2,1)} %bitcast.11, f32[16,384]{1,0:T(8,128)} %bitcast.14, f32[16,384]{1,0:T(8,128)} %bitcast.15, bf16[384,128]{1,0:T(8,128)(2,1)} %bitcast.12, ...), custom_call_target="tpu_custom_call" | custom-call | tf_op jit(solution)/shard_map/pallas_call | solution.py:425
  35.5 0.7 %shard_map.95 = (bf16[24,2,8,128]{3,2,1,0:T(8,128)(2,1)}, bf16[384,128]{1,0:T(8,128)(2,1)}, bf16[384,128]{1,0:T(8,128)(2,1)}) custom-call(bf16[24,2,8,128]{3,2,1,0:T(8,128)(2,1)S(1)} %get-tuple-element.8.dq_ref, bf16[2,384,128]{2,1,0:T(8,128)(2,1)S(1)} %get-tuple-element.9.dkv_ref), custom_call_target="tpu_custom_call" | custom-call | tf_op jit(solution)/shard_map/pallas_call | solution.py:492

commit v3 on v2

--- a/solution.py
+++ b/solution.py
@@ -327,11 +327,10 @@
     )
     to_sib.start()
 
-    forward(1, 0)
-    forward(2, 1)
-    for t in (3, 4, 5, 6):
-        for half in range(2):
-            forward(t, half)
+    for which in ((1, 0), (2, 1), (3, 1), (4, 0)):
+        forward(*which)
+    for which in ((3, 0), (4, 1), (5, 1), (6, 0)):
+        forward(*which)
 
     for k in range(1, PB):
         piece_arrival(k).wait_recv()
@@ -367,6 +366,9 @@
     @pl.when(owner != c)
     def _():
         spread_copy(0).start()
+
+    for which in ((5, 0), (6, 1)):
+        forward(*which)
 
     for side in range(2):
         for h in range(2):

time: 36.4 us -> 35.3 us (0.970)
  Pallas kernels: 35.6 us -> 34.5 us
    pallas_call x1, Pallas kernels: 34.9 us -> 33.8 us  [per_device(): pl.pallas_call(kernel, out_shape=(pltpu.VMEM((TOK // KA, 2, GROUP, D), BF...]
where the time goes in v3:
time: 35.3 us; the launch traced here: 35.1 us
  Pallas kernels  34.5 us (98%)
  between operations  0.64 us (2%)
    pallas_call x1, Pallas kernels, per_device(): pl.pallas_call(kernel, out_shape=(pltpu.VMEM((TOK // KA, 2, GROUP, D), BF...  33.8 us
    pallas_call x1, Pallas kernels, per_device(): pl.pallas_call(write_out, out_shape=(jax.ShapeDtypeStruct((TOK // KA, 2,...  0.73 us

profile of v3, /device:TPU:1, one launch (start us, length us, event | category | flops | bytes accessed | tf_op | source)
XLA Modules:
  0.0 35.1 jit_solution(1491955766511453731)
XLA Ops:
  0.6 33.8 %shard_map.94 = (bf16[24,2,8,128]{3,2,1,0:T(8,128)(2,1)S(1)}, bf16[2,384,128]{2,1,0:T(8,128)(2,1)S(1)}) custom-call(bf16[384,2,8,128]{3,2,1,0:T(8,128)(2,1)} %bitcast.10, bf16[384,2,8,128]{3,2,1,0:T(8,128)(2,1)} %bitcast.11, f32[16,384]{1,0:T(8,128)} %bitcast.14, f32[16,384]{1,0:T(8,128)} %bitcast.15, bf16[384,128]{1,0:T(8,128)(2,1)} %bitcast.12, ...), custom_call_target="tpu_custom_call" | custom-call | tf_op jit(solution)/shard_map/pallas_call | solution.py:427
  34.4 0.7 %shard_map.95 = (bf16[24,2,8,128]{3,2,1,0:T(8,128)(2,1)}, bf16[384,128]{1,0:T(8,128)(2,1)}, bf16[384,128]{1,0:T(8,128)(2,1)}) custom-call(bf16[24,2,8,128]{3,2,1,0:T(8,128)(2,1)S(1)} %get-tuple-element.8.dq_ref, bf16[2,384,128]{2,1,0:T(8,128)(2,1)S(1)} %get-tuple-element.9.dkv_ref), custom_call_target="tpu_custom_call" | custom-call | tf_op jit(solution)/shard_map/pallas_call | solution.py:494

commit v4 on v3

--- a/solution.py
+++ b/solution.py
@@ -47,8 +47,8 @@
     dq_ref, dkv_ref,
     tot_ref, dots_ref, codes_ref, vals_ref, pows_ref, merge,
     qbuf, gobuf, q2, go2, mbuf, deq, kv_full, sums, means, kt, s_all, dp_all,
-    stab, totf, gain, dqt, p_scr, ds_scr, dqbuf, acc, tx, rx, fin, sib, kvtx, kvrx, red, ag,
-    in_sem, kvx_s, kvx_r, mean_s, mean_r, tx_s, rx_r, fin_r, sib_r,
+    stab, totf, gain, dqt, p_scr, ds_scr, dqbuf, acc, tx, rx, far, fin, sib, kvtx, kvrx, red, ag,
+    in_sem, kvx_s, kvx_r, mean_s, mean_r, tx_s, rx_r, far_r, fin_r, sib_r,
     pb_s, pb_r, ag_s, ag_r,
 ):
     b = lax.axis_index("pb")
@@ -228,8 +228,14 @@
     def hop(t, half):
         leftward = half == 0 if t == 0 else t % 2 == 1
         to = left if leftward else right
+        if t == 0:
+            to = (z + NZ - 2) % NZ if leftward else (z + 2) % NZ
+            return pltpu.make_async_remote_copy(
+                src_ref=tx.at[t, half], dst_ref=far.at[half], send_sem=tx_s.at[t, half],
+                recv_sem=far_r.at[half], device_id={"ka": 2 * to + c}, device_id_type=MESH,
+            )
         if t < 5:
-            at = (1 if half == 0 else 2) if t == 0 else t + 2
+            at = t + 2
             return pltpu.make_async_remote_copy(
                 src_ref=tx.at[t, half], dst_ref=rx.at[at, half], send_sem=tx_s.at[t, half],
                 recv_sem=rx_r.at[at, half], device_id={"ka": 2 * to + c}, device_id_type=MESH,
@@ -246,6 +252,12 @@
             recv_sem=rx_r.at[t, half], device_id={"ka": sibling}, device_id_type=MESH,
         )
 
+    def far_arrival(half):
+        return pltpu.make_async_remote_copy(
+            src_ref=tx.at[0, half], dst_ref=far.at[half], send_sem=tx_s.at[0, half],
+            recv_sem=far_r.at[half], device_id={"ka": sibling}, device_id_type=MESH,
+        )
+
     def part(t, half):
         return dqbuf[t, half * HALF:(half + 1) * HALF, :]
 
@@ -255,7 +267,11 @@
 
     def forward(t, half):
         arrival(t, half).wait_recv()
-        tx[t, half] = (part(t, half) + rx[t, half].astype(F32)).astype(BF16)
+        summed = part(t, half) + rx[t, half].astype(F32)
+        if (t, half) in ((3, 0), (4, 1)):
+            far_arrival(half).wait_recv()
+            summed = summed + far[half].astype(F32)
+        tx[t, half] = summed.astype(BF16)
         hop(t, half).start()
 
     def finish_share(t):
@@ -274,10 +290,9 @@
         if t == 0:
             begin(0, 0)
             begin(0, 1)
-        elif t == 1:
-            begin(1, 1)
-        elif t == 2:
-            begin(2, 0)
+        elif t < 3:
+            begin(t, 0)
+            begin(t, 1)
 
     def second(i, carry):
         places = []
@@ -327,9 +342,7 @@
     )
     to_sib.start()
 
-    for which in ((1, 0), (2, 1), (3, 1), (4, 0)):
-        forward(*which)
-    for which in ((3, 0), (4, 1), (5, 1), (6, 0)):
+    for which in ((3, 1), (4, 0), (3, 0), (4, 1)):
         forward(*which)
 
     for k in range(1, PB):
@@ -367,7 +380,7 @@
     def _():
         spread_copy(0).start()
 
-    for which in ((5, 0), (6, 1)):
+    for which in ((5, 1), (6, 0), (5, 0), (6, 1)):
         forward(*which)
 
     for side in range(2):
@@ -461,6 +474,7 @@
             pltpu.VMEM((2, CKEYS, D), F32),
             pltpu.VMEM((NZ, 2, HALF, D), BF16),
             pltpu.VMEM((7, 2, HALF, D), BF16),
+            pltpu.VMEM((2, HALF, D), BF16),
             pltpu.VMEM((2, 2, HALF, D), BF16),
             pltpu.VMEM((HALF, D), BF16),
             pltpu.VMEM((2, CKEYS, D), BF16),
@@ -474,6 +488,7 @@
             dma((KA,)),
             dma((NZ, 2)),
             dma((7, 2)),
+            dma((2,)),
             dma((2, 2)),
             dma,
             dma((PB,)),

time: 35.3 us -> 34.6 us (0.980)
  Pallas kernels: 34.5 us -> 33.8 us
    pallas_call x1, Pallas kernels: 33.8 us -> 33.1 us  [per_device(): pl.pallas_call(kernel, out_shape=(pltpu.VMEM((TOK // KA, 2, GROUP, D), BF...]
where the time goes in v4:
time: 34.6 us; the launch traced here: 34.5 us
  Pallas kernels  33.8 us (98%)
  between operations  0.64 us (2%)
    pallas_call x1, Pallas kernels, per_device(): pl.pallas_call(kernel, out_shape=(pltpu.VMEM((TOK // KA, 2, GROUP, D), BF...  33.1 us
    pallas_call x1, Pallas kernels, per_device(): pl.pallas_call(write_out, out_shape=(jax.ShapeDtypeStruct((TOK // KA, 2,...  0.73 us

profile of v4, /device:TPU:1, one launch (start us, length us, event | category | flops | bytes accessed | tf_op | source)
XLA Modules:
  0.0 34.5 jit_solution(19497317235410776)
XLA Ops:
  0.6 33.1 %shard_map.94 = (bf16[24,2,8,128]{3,2,1,0:T(8,128)(2,1)S(1)}, bf16[2,384,128]{2,1,0:T(8,128)(2,1)S(1)}) custom-call(bf16[384,2,8,128]{3,2,1,0:T(8,128)(2,1)} %bitcast.10, bf16[384,2,8,128]{3,2,1,0:T(8,128)(2,1)} %bitcast.11, f32[16,384]{1,0:T(8,128)} %bitcast.14, f32[16,384]{1,0:T(8,128)} %bitcast.15, bf16[384,128]{1,0:T(8,128)(2,1)} %bitcast.12, ...), custom_call_target="tpu_custom_call" | custom-call | tf_op jit(solution)/shard_map/pallas_call | solution.py:440
  33.7 0.7 %shard_map.95 = (bf16[24,2,8,128]{3,2,1,0:T(8,128)(2,1)}, bf16[384,128]{1,0:T(8,128)(2,1)}, bf16[384,128]{1,0:T(8,128)(2,1)}) custom-call(bf16[24,2,8,128]{3,2,1,0:T(8,128)(2,1)S(1)} %get-tuple-element.8.dq_ref, bf16[2,384,128]{2,1,0:T(8,128)(2,1)S(1)} %get-tuple-element.9.dkv_ref), custom_call_target="tpu_custom_call" | custom-call | tf_op jit(solution)/shard_map/pallas_call | solution.py:509

commit v5 on v4

--- a/solution.py
+++ b/solution.py
@@ -274,25 +274,27 @@
         tx[t, half] = summed.astype(BF16)
         hop(t, half).start()
 
-    def finish_share(t):
+    def find_gain(t):
         s = (z + offset(t) + NZ) % NZ
         rows = pl.ds(pl.multiple_of(s * ROWS, ROWS), ROWS)
         shift = jnp.sum(dot(mean_rows, q2[rows, :], NT)[0:8], axis=0, keepdims=True)
-        factor = jnp.exp2(stab[s] - shift * (inv * LOG2E))
-        gain[s] = factor
+        gain[s] = jnp.exp2(stab[s] - shift * (inv * LOG2E))
+
+    def finish_share(t):
+        s = (z + offset(t) + NZ) % NZ
+        factor = gain[s]
         for l0 in range(0, ROWS, D):
             at = slice(l0, l0 + D)
             centred = dqt[s, :, at] - mean_col * totf[s, :, at]
             dqbuf[t, at, :] = (centred * (factor[:, at] * inv)).T
 
-    for t in range(NZ):
+    for t in range(3):
+        find_gain(t)
         finish_share(t)
-        if t == 0:
-            begin(0, 0)
-            begin(0, 1)
-        elif t < 3:
-            begin(t, 0)
-            begin(t, 1)
+        begin(t, 0)
+        begin(t, 1)
+    for t in range(3, NZ):
+        find_gain(t)
 
     def second(i, carry):
         places = []
@@ -333,6 +335,9 @@
 
     for k in range(1, PB):
         piece_copy(k).start()
+
+    for t in range(3, NZ):
+        finish_share(t)
 
     tx[7, 0] = part(7, 0).astype(BF16)
     tx[7, 1] = part(7, 1).astype(BF16)

time: 34.6 us -> 34.6 us (level)
  no operation moved by 1% of the time
where the time goes in v5:
time: 34.6 us; the launch traced here: 34.5 us
  Pallas kernels  33.8 us (98%)
  between operations  0.64 us (2%)
    pallas_call x1, Pallas kernels, per_device(): pl.pallas_call(kernel, out_shape=(pltpu.VMEM((TOK // KA, 2, GROUP, D), BF...  33.1 us
    pallas_call x1, Pallas kernels, per_device(): pl.pallas_call(write_out, out_shape=(jax.ShapeDtypeStruct((TOK // KA, 2,...  0.73 us

profile of v5, /device:TPU:1, one launch (start us, length us, event | category | flops | bytes accessed | tf_op | source)
XLA Modules:
  0.0 34.5 jit_solution(7201378300707096123)
XLA Ops:
  0.6 33.1 %shard_map.94 = (bf16[24,2,8,128]{3,2,1,0:T(8,128)(2,1)S(1)}, bf16[2,384,128]{2,1,0:T(8,128)(2,1)S(1)}) custom-call(bf16[384,2,8,128]{3,2,1,0:T(8,128)(2,1)} %bitcast.10, bf16[384,2,8,128]{3,2,1,0:T(8,128)(2,1)} %bitcast.11, f32[16,384]{1,0:T(8,128)} %bitcast.14, f32[16,384]{1,0:T(8,128)} %bitcast.15, bf16[384,128]{1,0:T(8,128)(2,1)} %bitcast.12, ...), custom_call_target="tpu_custom_call" | custom-call | tf_op jit(solution)/shard_map/pallas_call | solution.py:445
  33.7 0.7 %shard_map.95 = (bf16[24,2,8,128]{3,2,1,0:T(8,128)(2,1)}, bf16[384,128]{1,0:T(8,128)(2,1)}, bf16[384,128]{1,0:T(8,128)(2,1)}) custom-call(bf16[24,2,8,128]{3,2,1,0:T(8,128)(2,1)S(1)} %get-tuple-element.8.dq_ref, bf16[2,384,128]{2,1,0:T(8,128)(2,1)S(1)} %get-tuple-element.9.dkv_ref), custom_call_target="tpu_custom_call" | custom-call | tf_op jit(solution)/shard_map/pallas_call | solution.py:514
